TPU v7x, 32 devices: a whole 2x2x4 slice. The times are simulated.
32 devices in a mesh: seq: 16 (over z, y, core), exp: 2 (over x).
Axes of the slice: x: 2, y: 2, z: 4, core: 2. Of those that a mesh axis runs over, the one named last changes fastest.
Arguments:
- hidden_in: bfloat16 [6, 6144], P('exp', 'seq'), may hold values from -2 to 2
- queries: bfloat16 [6, 6144], P(None, 'exp'), may hold values from -40 to 40
- key_cache: bfloat16 [6, 8192, 1024], P(None, 'seq', 'exp'), may hold values from -16 to 16
- value_cache: bfloat16 [6, 8192, 1024], P(None, 'seq', 'exp'), may hold values from -6 to 6
- lengths: int32 [6], replicated, may hold values from 2 to 8192
- out_weight: bfloat16 [6144, 6144], P('exp', 'seq'), may hold values from -0.078125 to 0.078125
- norm_gain: float32 [6144], P('seq'), may hold values from 0.1 to 1.9
- router: bfloat16 [6144, 8], P('seq'), may hold values from -0.078125 to 0.078125
- expert_ids: int32 [6, 2], P('exp'), may hold values from 0 to 7, as said below
- capacity: int32 [8], replicated, may hold values from 1 to 3, as said below
- w_gate: bfloat16 [8, 6144, 8192], P('exp', None, 'seq'), may hold values from -0.078125 to 0.078125
- w_up: bfloat16 [8, 6144, 8192], P('exp', None, 'seq'), may hold values from -0.078125 to 0.078125
- w_down: bfloat16 [8, 8192, 6144], P('exp', 'seq'), may hold values from -0.09375 to 0.09375
Outputs:
- layer_out: bfloat16 [6, 6144], P('exp', 'seq')
Inputs may be any that keep to these rules, and one draw needn't show every extreme that they name: lengths[b] counts sequence b's live cache positions, the newest token's included. `expert_ids`: the two experts of a token differ. One expert is named by every token; any other expert is named at most 3 times within one aligned block of 3 tokens. The expert that every token names has capacity 3.
All inputs are finite; a program needn't handle non-finite values.
Results may differ from a plain program's by a relative error of at most 0.0085.
Values may be sent and summed in bfloat16 or wider, within the bound.
A program may use at most 128 MiB of HBM per device.

v0:
```python
import math
import jax
import jax.numpy as jnp
from jax import lax
from jax.sharding import PartitionSpec as P

D = 6144
HEADS = 48
KV_HEADS = 8
HEAD_DIM = 128
EXPERTS = 8
masked_score = -1e30
norm_eps = 1e-05


def joined(value, axis, join):
    pieces = jax.tree.map(lambda part: lax.all_gather(part, axis), value)
    head = jax.tree.map(lambda part: part[0], pieces)
    tail = jax.tree.map(lambda part: part[1:], pieces)
    running, _ = lax.scan(lambda running, share: (join(running, share), None), head, tail)
    return running


def merge_partial_results(left_part, right_part):
    left_maximum_score, left_denom, left_sum = left_part
    right_peak, right_denom, right_sum = right_part
    joint_peak = jnp.maximum(left_maximum_score, right_peak)
    left_factor = jnp.exp(left_maximum_score - joint_peak)
    right_factor = jnp.exp(right_peak - joint_peak)
    return (
        joint_peak,
        left_denom * left_factor + right_denom * right_factor,
        left_sum * left_factor[..., None] + right_sum * right_factor[..., None],
    )


def on_device(
    hidden_in,
    queries,
    key_cache,
    value_cache,
    lengths,
    out_weight,
    norm_gain,
    router,
    expert_ids,
    capacity,
    w_gate,
    w_up,
    w_down,
):
    seq_count = queries.shape[0]
    group_size = HEADS // KV_HEADS
    kv_local = key_cache.shape[2] // HEAD_DIM
    span_local = key_cache.shape[1]
    query_heads = queries.reshape(seq_count, kv_local, group_size, HEAD_DIM)
    key_rows = key_cache.reshape(seq_count, span_local, kv_local, HEAD_DIM)
    value_rows = value_cache.reshape(seq_count, span_local, kv_local, HEAD_DIM).astype(jnp.float32)
    first_place = lax.axis_index("seq") * span_local
    places = first_place + jnp.arange(span_local, dtype=jnp.int32)
    live_mask = (places[None, :] < lengths[:, None])[:, None, None, :]
    scores = jnp.einsum(
        "bkgd,bjkd->bkgj", query_heads, key_rows, preferred_element_type=jnp.float32
    ) * (1.0 / math.sqrt(HEAD_DIM))
    scores = jnp.where(live_mask, scores, masked_score)
    local_peak = jnp.max(scores, axis=-1)
    attn_weights = jnp.where(live_mask, jnp.exp(scores - local_peak[..., None]), 0.0)
    local_sum = jnp.einsum(
        "bkgj,bjkd->bkgd", attn_weights, value_rows, precision=lax.Precision.HIGHEST
    )
    global_peak, denom_sum, weighted = joined(
        (local_peak, jnp.sum(attn_weights, axis=-1), local_sum), "seq", merge_partial_results
    )
    attended = (
        (weighted / denom_sum[..., None])
        .reshape(seq_count, kv_local * group_size * HEAD_DIM)
        .astype(jnp.bfloat16)
    )
    partial_value = jnp.dot(attended, out_weight, preferred_element_type=jnp.float32)
    projected = lax.psum_scatter(partial_value, "exp", scatter_dimension=0, tiled=True)
    residual = hidden_in.astype(jnp.float32) + projected
    gained = residual * norm_gain
    router_wide = router.astype(jnp.float32)
    squares = jnp.sum(residual * residual, axis=-1)
    total_sq = lax.psum(squares, "seq")
    scale_row = lax.rsqrt(total_sq / D + norm_eps)
    logits = lax.psum(
        jnp.dot(gained * scale_row[:, None], router_wide, precision=lax.Precision.HIGHEST), "seq"
    )
    normed = (gained * scale_row[:, None]).astype(jnp.bfloat16)
    row_total = expert_ids.shape[0]
    onehot_int = (
        expert_ids[:, :, None] == jnp.arange(EXPERTS, dtype=jnp.int32)[None, None, :]
    ).astype(jnp.int32)
    name_count = jnp.sum(onehot_int, axis=1)
    row_order = jnp.arange(row_total, dtype=jnp.int32)
    before = (row_order[None, :] < row_order[:, None]).astype(jnp.int32)
    earlier = jnp.dot(before, name_count)
    slot_rank = jnp.sum(onehot_int * earlier[:, None, :], axis=-1)
    slot_limit = jnp.sum(onehot_int * capacity[None, None, :], axis=-1)
    kept_mask = (slot_rank < slot_limit).astype(jnp.float32)
    expert_indicator = onehot_int.astype(jnp.float32)
    chosen = jnp.sum(expert_indicator * logits[:, None, :], axis=-1)
    gate_weight = jax.nn.sigmoid(chosen - chosen[:, ::-1])
    slot_match = (slot_rank[:, :, None] == row_order[None, None, :]).astype(jnp.float32)
    placing = jnp.einsum("rke,rks->esr", expert_indicator * kept_mask[:, :, None], slot_match)
    buffer = jnp.einsum(
        "esr,rd->esd", placing.astype(jnp.bfloat16), normed, preferred_element_type=jnp.float32
    ).astype(jnp.bfloat16)
    dispatched = lax.all_to_all(buffer, "exp", split_axis=0, concat_axis=1, tiled=True)
    shard_rows = lax.all_gather(dispatched, "seq", axis=2, tiled=True)
    gate_next = jnp.einsum("ern,enf->erf", shard_rows, w_gate, preferred_element_type=jnp.float32)
    up_next = jnp.einsum("ern,enf->erf", shard_rows, w_up, preferred_element_type=jnp.float32)
    hidden_act = (jax.nn.silu(gate_next) * up_next).astype(jnp.bfloat16)
    partial_out = jnp.einsum("erf,efd->erd", hidden_act, w_down, preferred_element_type=jnp.float32)
    blend_table = jnp.einsum(
        "rke,rks->esr", expert_indicator * (gate_weight * kept_mask)[:, :, None], slot_match
    )
    reduced_output = lax.psum_scatter(partial_out, "seq", scatter_dimension=2, tiled=True)
    returned = lax.all_to_all(reduced_output, "exp", split_axis=1, concat_axis=0, tiled=True)
    combined = jnp.einsum("esr,esd->rd", blend_table, returned, precision=lax.Precision.HIGHEST)
    return (residual + combined).astype(jnp.bfloat16)


def solution(mesh):
    in_specs = (
        P("exp", "seq"),
        P(None, "exp"),
        P(None, "seq", "exp"),
        P(None, "seq", "exp"),
        P(),
        P("exp", "seq"),
        P("seq"),
        P("seq", None),
        P("exp", None),
        P(),
        P("exp", None, "seq"),
        P("exp", None, "seq"),
        P("exp", "seq", None),
    )
    out_specs = P("exp", "seq")
    return jax.shard_map(
        on_device, mesh=mesh, in_specs=in_specs, out_specs=out_specs, check_vma=False
    )
```

profile of v0, /device:TPU:0, one launch (start us, length us, event | category | flops | bytes accessed | tf_op | source)
XLA Modules:
  0.0 272.3 jit_solution(8240845647066863271)
XLA Ops:
  6.5 1.6 reshape.56
  8.2 0.9 broadcast_compare_fusion
  9.1 1.8 fusion.49
  10.9 1.4 fusion.4
  12.3 0.7 copy.28
  13.1 23.7 %all-gather = f32[96,4,6]{2,1,0:T(4,128)S(1)} all-gather(f32[6,4,6]{2,1,0:T(4,128)S(1)} %get-tuple-element.74), channel_id=2, replica_groups=mesh['seq'=16,'exp'=2] {'seq'}, dimensions={0}, use_global_device_ids=true | all-gather | bytes 9792 | tf_op jit(solution)/shard_map/all_gather | solution.py:17
  36.8 0.2 fusion.20
  37.0 18.4 %all-gather.1 = f32[96,4,6]{2,1,0:T(4,128)S(1)} all-gather(f32[6,4,6]{2,1,0:T(4,128)S(1)} %fusion.20), channel_id=3, replica_groups=mesh['seq'=16,'exp'=2] {'seq'}, dimensions={0}, use_global_device_ids=true | all-gather | bytes 9792 | tf_op jit(solution)/shard_map/all_gather | solution.py:17
  55.5 0.7 dynamic-slice
  57.0 0.9 slice.32
  57.9 2.3 slice.35
  60.3 16.4 %while.14 = (s32[]{:T(128)}, f32[6,4,6]{2,1,0:T(4,128)S(1)}, f32[6,4,6]{2,1,0:T(4,128)S(1)}, f32[6,4,6,128]{3,2,1,0:T(8,128)S(1)}, f32[15,6,4,6]{3,2,1,0:T(4,128...) while((s32[]{:T(128)}, f32[6,4,6]{2,1,0:T(4,128)S(1)}, ...), condition=%wide.region_3.4_spmd, body=%wide.region_2.3_spmd.sunk | while | flops 56162 | bytes 374501 | solution.py:20
  60.3 0.9 constant_dynamic-slice_fusion.2
  61.2 0.1 fusion.70
  61.4 0.9 constant_dynamic-slice_fusion.2
  62.3 0.1 fusion.70
  62.5 0.9 constant_dynamic-slice_fusion.2
  63.4 0.1 fusion.70
  63.6 0.9 constant_dynamic-slice_fusion.2
  64.5 0.1 fusion.70
  64.7 0.9 constant_dynamic-slice_fusion.2
  65.6 0.1 fusion.70
  65.8 0.9 constant_dynamic-slice_fusion.2
  66.7 0.1 fusion.70
  66.9 0.9 constant_dynamic-slice_fusion.2
  67.7 0.1 fusion.70
  67.9 0.9 constant_dynamic-slice_fusion.2
  68.8 0.1 fusion.70
  69.0 0.9 constant_dynamic-slice_fusion.2
  69.9 0.1 fusion.70
  70.1 0.9 constant_dynamic-slice_fusion.2
  71.0 0.1 fusion.70
  71.2 0.9 constant_dynamic-slice_fusion.2
  72.1 0.1 fusion.70
  72.3 0.9 constant_dynamic-slice_fusion.2
  73.2 0.1 fusion.70
  73.4 0.9 constant_dynamic-slice_fusion.2
  74.3 0.1 fusion.70
  74.5 0.9 constant_dynamic-slice_fusion.2
  75.4 0.1 fusion.70
  75.6 0.9 constant_dynamic-slice_fusion.2
  76.5 0.1 fusion.70
  76.8 0.4 fusion.50
  77.2 8.1 %all-reduce = f32[6,384]{1,0:T(8,128)S(1)} all-reduce(f32[6,384]{1,0:T(8,128)S(1)} %fusion.50), channel_id=5, replica_groups=mesh['seq'=16,'exp'=2] {'exp'}, use_global_device_ids=true, to_apply=%region_4.5.clone | all-reduce | flops 2304 | bytes 18432
  85.3 0.1 multiply_reduce_fusion
  85.4 0.1 fusion.40
  85.5 29.5 %psum.14 = f32[3]{0:T(128)S(1)} all-reduce(f32[3]{0:T(128)S(1)} %multiply_reduce_fusion), channel_id=1, replica_groups=mesh['seq'=16,'exp'=2] {'seq'}, use_global_device_ids=true, to_apply=%region_9.10 | all-reduce | flops 3 | bytes 24 | tf_op jit(solution)/shard_map/psum | solution.py:85
  115.0 0.2 fusion.26
  115.2 0.3 select_reduce_fusion
  115.5 29.5 %psum.15 = f32[3,8]{1,0:T(4,128)S(1)} all-reduce(f32[3,8]{1,0:T(4,128)S(1)} %fusion.26), channel_id=1, replica_groups=mesh['seq'=16,'exp'=2] {'seq'}, use_global_device_ids=true, to_apply=%region_10.11 | all-reduce | flops 24 | bytes 192 | tf_op jit(solution)/shard_map/psum | solution.py:87
  145.0 0.2 fusion.30
  145.2 0.3 fusion.19
  145.5 0.2 convolution_convert_fusion
  145.7 6.3 %all_to_all.36 = bf16[8,3,384]{2,1,0:T(4,128)(2,1)S(1)} all-to-all(bf16[8,3,384]{2,1,0:T(4,128)(2,1)S(1)} %copy.33), channel_id=1, replica_groups=mesh['seq'=16,'exp'=2] {'exp'}, dimensions={0} | all-to-all | bytes 36864 | tf_op jit(solution)/shard_map/all_to_all | solution.py:110
  152.0 18.3 %all_gather.27 = bf16[4,6,6144]{2,1,0:T(8,128)(2,1)S(1)} all-gather(bf16[4,6,384]{2,1,0:T(8,128)(2,1)S(1)} %copy.35), channel_id=1, replica_groups=mesh['seq'=16,'exp'=2] {'seq'}, dimensions={2}, use_global_device_ids=true | all-gather | bytes 313344 | tf_op jit(solution)/shard_map/all_gather | solution.py:111
  170.3 9.9 %fusion.51 = f32[4,6,512]{2,1,0:T(8,128)S(1)} fusion(bf16[4,6,6144]{2,1,0:T(8,128)(2,1)S(1)} %all_gather.27, bf16[4,6144,512]{2,1,0:T(8,128)(2,1)} %param.25), kind=kOutput, calls=%fused_computation.70 | convolution fusion | flops 150994944 | bytes 25509888 | tf_op jit(solution)/shard_map/ern,enf->erf/dot_general | solution.py:112
  180.2 9.9 %fusion.16 = bf16[4,6,512]{2,1,0:T(8,128)(2,1)S(1)} fusion(bf16[4,6,6144]{2,1,0:T(8,128)(2,1)S(1)} %all_gather.27, bf16[4,6144,512]{2,1,0:T(8,128)(2,1)} %param.26, f32[4,6,512]{2,1,0:T(8,128)S(1)} %fusion.51), kind=kOutput, calls=%fused_computation.19 | convolution fusion | flops 151068672 | bytes 25534464 | tf_op jit(solution)/shard_map/ern,enf->erf/dot_general | solution.py:113
  190.1 10.9 %fusion.52 = f32[4,6,6144]{2,1,0:T(8,128)} fusion(bf16[4,6,512]{2,1,0:T(8,128)(2,1)S(1)} %fusion.16, bf16[4,512,6144]{2,1,0:T(8,128)(2,1)} %param.27), kind=kOutput, calls=%fused_computation.71 | convolution fusion | flops 150994944 | bytes 25780224 | tf_op jit(solution)/shard_map/erf,efd->erd/dot_general | solution.py:115
  201.1 54.9 %reduce-scatter.2.cloned.1.call-done = f32[4,6,384]{2,1,0:T(8,128)} async-done(((f32[4,6,6144]{2,1,0:T(8,128)}), f32[4,6,384]{2,1,0:T(8,128)}) %reduce-scatter.2.cloned.1.call-update) | async-done | bytes 36880 | tf_op jit(solution)/shard_map/reduce_scatter | solution.py:119
  255.9 1.4 copy.36
  257.4 3.3 %all-to-all-start.1 = ((f32[4,6,384]{2,0,1:T(4,128)}), f32[4,6,384]{2,0,1:T(4,128)S(1)}, u32[]{:S(2)}, u32[]{:S(2)}) async-start(f32[4,6,384]{2,0,1:T(4,128)} %copy.36), calls=%async_computation.2 | async-start | bytes 73728 | tf_op jit(solution)/shard_map/all_to_all | solution.py:120
  260.6 0.3 convolution_bitcast_fusion.1
  260.9 3.7 %all-to-all-done.1 = f32[4,6,384]{2,0,1:T(4,128)S(1)} async-done(((f32[4,6,384]{2,0,1:T(4,128)}), f32[4,6,384]{2,0,1:T(4,128)S(1)}, u32[]{:S(2)}, u32[]{:S(2)}) %all-to-all-start.1) | async-done | bytes 36896 | tf_op jit(solution)/shard_map/all_to_all | solution.py:120
  264.6 0.8 fusion.18
  (59 shorter events, 1.2 us)
Async XLA Ops:
  6.5 2.5 copy-start
  6.5 50.4 %all-gather.5.cloned.1.call-start = ((), (), s32[]{:S(2)}) async-start(), calls=%async_computation.4 | async-start | bytes 1253376 | tf_op jit(solution)/shard_map/all_gather | solution.py:17
  8.2 2.7 %copy-start.2 = (bf16[6,512,512]{2,1,0:T(8,128)(2,1)S(1)}, bf16[6,512,512]{2,1,0:T(8,128)(2,1)}, u32[]{:S(2)}) copy-start(bf16[6,512,512]{2,1,0:T(8,128)(2,1)} %param.18) | copy-start | bytes 9437188
  10.9 44.5 %copy-start.5 = (s32[3,2]{0,1:T(2,128)S(1)}, s32[3,2]{0,1:T(2,128)}, u32[]{:S(2)}) copy-start(s32[3,2]{0,1:T(2,128)} %param.23) | copy-start | bytes 76
  10.9 44.6 %copy-start.9 = (u32[32]{0:T(128)S(1)}, u32[32]{0:T(128)}, u32[]{:S(2)}) copy-start(u32[32]{0:T(128)} %constant.44) | copy-start | bytes 388
  13.0 242.9 %reduce-scatter.2.cloned.1.call-start = ((), (), s32[]{:S(2)}) async-start(), calls=%async_computation.3 | async-start | bytes 835584 | tf_op jit(solution)/shard_map/reduce_scatter | solution.py:119
  37.0 39.8 %copy-start.3 = (bf16[3072,384]{1,0:T(8,128)(2,1)S(1)}, bf16[3072,384]{1,0:T(8,128)(2,1)}, u32[]{:S(2)}) copy-start(bf16[3072,384]{1,0:T(8,128)(2,1)} %param.20) | copy-start | bytes 7077892
  60.2 25.0 %copy-start.4 = (bf16[3,384]{1,0:T(4,128)(2,1)S(1)}, bf16[3,384]{1,0:T(4,128)(2,1)}, u32[]{:S(2)}) copy-start(bf16[3,384]{1,0:T(4,128)(2,1)} %param.15) | copy-start | bytes 6916
  60.3 54.8 %copy-start.7 = (bf16[384,8]{0,1:T(8,128)(2,1)S(1)}, bf16[384,8]{0,1:T(8,128)(2,1)}, u32[]{:S(2)}) copy-start(bf16[384,8]{0,1:T(8,128)(2,1)} %param.22) | copy-start | bytes 18436
  60.3 54.8 %copy-start.8 = (f32[384]{0:T(512)S(1)}, f32[384]{0:T(512)}, u32[]{:S(2)}) copy-start(f32[384]{0:T(512)} %param.21) | copy-start | bytes 4612
  60.3 55.0 %copy-start.6 = (s32[8]{0:T(128)S(1)}, s32[8]{0:T(128)}, u32[]{:S(2)}) copy-start(s32[8]{0:T(128)} %param.24) | copy-start | bytes 100
  190.1 75.3 %copy-start.1 = (bf16[6,512,512]{2,1,0:T(8,128)(2,1)S(1)}, bf16[6,512,512]{2,1,0:T(8,128)(2,1)}, u32[]{:S(2)}) copy-start(bf16[6,512,512]{2,1,0:T(8,128)(2,1)} %param.17) | copy-start | bytes 9437188
  257.4 7.2 %all-to-all-start.1 = ((f32[4,6,384]{2,0,1:T(4,128)}), f32[4,6,384]{2,0,1:T(4,128)S(1)}, u32[]{:S(2)}, u32[]{:S(2)}) async-start(f32[4,6,384]{2,0,1:T(4,128)} %copy.36), calls=%async_computation.2 | async-start | bytes 73728 | tf_op jit(solution)/shard_map/all_to_all | solution.py:120
Sparse Core Ops, SparseCore 0:
  13.1 41.2 all-gather.4
  201.2 54.6 reduce-scatter.1
where the time goes:
time: 273 us; the launch traced here: 272 us
  blocking collectives  134 us (49%)
  waiting for transfers between devices  58.6 us (21%)
  matrix products  36.3 us (13%)
  local copies, waits for them, and re-layouts  21.4 us (8%)
  between operations  14.3 us (5%)
  other arithmetic  4.47 us (2%)
  starting transfers between devices  3.3 us (1%)
    reduce_scatter x1, waiting for transfers between devices, on_device(): lax.psum_scatter(partial_out, 'seq', scatter_dimension=2, tiled=True)  54.9 us
    all_gather x2, blocking collectives, joined(): pieces = jax.tree.map(lambda part: lax.all_gather(part, axis), value)  42.1 us
    psum x1, blocking collectives, on_device(): lax.psum(jnp.dot(gained * scale_row[:, None], router_wide, precision=lax....  29.5 us
    psum x1, blocking collectives, on_device(): total_sq = lax.psum(squares, 'seq')  29.5 us
    all_gather x1, blocking collectives, on_device(): shard_rows = lax.all_gather(dispatched, 'seq', axis=2, tiled=True)  18.3 us
    dynamic_slice x15, local copies, waits for them, and re-layouts, joined(): lax.scan(lambda running, share: (join(running, share), None), head, tail)  13.4 us
    dot_general x1, matrix products, on_device(): jnp.einsum('erf,efd->erd', hidden_act, w_down, preferred_element_type=jnp...  10.9 us
    dot_general x1, matrix products, on_device(): jnp.einsum('ern,enf->erf', shard_rows, w_up, preferred_element_type=jnp.f...  9.94 us
  transfers between devices with their start and end apart: 3, of which 2 were waited for; matrix products, arithmetic and copies ran while one was open for 1% of the time, Pallas kernels for 0%

commit v1 on v0

--- a/solution.py
+++ b/solution.py
@@ -82,7 +82,10 @@
     gained = residual * norm_gain
     router_wide = router.astype(jnp.float32)
     squares = jnp.sum(residual * residual, axis=-1)
-    total_sq = lax.psum(squares, "seq")
+    size, total_sq = (lax.axis_size("seq"), squares)
+    for stride in [1 << k for k in range(size.bit_length() - 1)]:
+        pairs = [(i, i ^ stride) for i in range(size)]
+        total_sq = total_sq + lax.ppermute(total_sq, "seq", pairs)
     scale_row = lax.rsqrt(total_sq / D + norm_eps)
     logits = lax.psum(
         jnp.dot(gained * scale_row[:, None], router_wide, precision=lax.Precision.HIGHEST), "seq"

time: 273 us -> 257 us (0.941)
  blocking collectives: 134 us -> 104 us
  waiting for transfers between devices: 58.6 us -> 69.5 us
    psum x1 -> x0, blocking collectives: 29.5 us -> none  [on_device(): total_sq = lax.psum(squares, 'seq')]
    ppermute x0 -> x4, waiting for transfers between devices: none -> 11 us  [on_device(): total_sq = total_sq + lax.ppermute(total_sq, 'seq', pairs)]
  transfers between devices with their start and end apart: 3 -> 7, of which waited for: 2 -> 6; matrix products, arithmetic and copies ran while one was open for 1% -> 1% of each run, Pallas kernels for 0% -> 0%
where the time goes in v1:
time: 257 us; the launch traced here: 256 us
  blocking collectives  104 us (40%)
  waiting for transfers between devices  69.5 us (27%)
  matrix products  36.3 us (14%)
  local copies, waits for them, and re-layouts  21.4 us (8%)
  between operations  14.3 us (6%)
  starting transfers between devices  5.17 us (2%)
  other arithmetic  4.48 us (2%)
    reduce_scatter x1, waiting for transfers between devices, on_device(): lax.psum_scatter(partial_out, 'seq', scatter_dimension=2, tiled=True)  54.9 us
    all_gather x2, blocking collectives, joined(): pieces = jax.tree.map(lambda part: lax.all_gather(part, axis), value)  42.1 us
    psum x1, blocking collectives, on_device(): lax.psum(jnp.dot(gained * scale_row[:, None], router_wide, precision=lax....  29.5 us
    all_gather x1, blocking collectives, on_device(): shard_rows = lax.all_gather(dispatched, 'seq', axis=2, tiled=True)  18.3 us
    dynamic_slice x15, local copies, waits for them, and re-layouts, joined(): lax.scan(lambda running, share: (join(running, share), None), head, tail)  13.4 us
    ppermute x4, waiting for transfers between devices, on_device(): total_sq = total_sq + lax.ppermute(total_sq, 'seq', pairs)  11 us
    dot_general x1, matrix products, on_device(): jnp.einsum('erf,efd->erd', hidden_act, w_down, preferred_element_type=jnp...  10.9 us
    dot_general x1, matrix products, on_device(): jnp.einsum('ern,enf->erf', shard_rows, w_up, preferred_element_type=jnp.f...  9.94 us
  transfers between devices with their start and end apart: 7, of which 6 were waited for; matrix products, arithmetic and copies ran while one was open for 1% of the time, Pallas kernels for 0%

profile of v1, /device:TPU:0, one launch (start us, length us, event | category | flops | bytes accessed | tf_op | source)
XLA Modules:
  0.0 255.7 jit_solution(8989080062421339325)
XLA Ops:
  6.5 1.6 reshape.56
  8.2 0.9 broadcast_compare_fusion
  9.1 1.8 fusion.49
  10.9 1.4 fusion.4
  12.3 0.7 copy.28
  13.1 23.7 %all-gather = f32[96,4,6]{2,1,0:T(4,128)S(1)} all-gather(f32[6,4,6]{2,1,0:T(4,128)S(1)} %get-tuple-element.74), channel_id=2, replica_groups=mesh['seq'=16,'exp'=2] {'seq'}, dimensions={0}, use_global_device_ids=true | all-gather | bytes 9792 | tf_op jit(solution)/shard_map/all_gather | solution.py:17
  36.8 0.2 fusion.20
  37.0 18.4 %all-gather.1 = f32[96,4,6]{2,1,0:T(4,128)S(1)} all-gather(f32[6,4,6]{2,1,0:T(4,128)S(1)} %fusion.20), channel_id=3, replica_groups=mesh['seq'=16,'exp'=2] {'seq'}, dimensions={0}, use_global_device_ids=true | all-gather | bytes 9792 | tf_op jit(solution)/shard_map/all_gather | solution.py:17
  55.5 0.7 dynamic-slice
  57.1 0.9 slice.32
  58.0 2.3 slice.35
  60.4 16.4 %while.14 = (s32[]{:T(128)}, f32[6,4,6]{2,1,0:T(4,128)S(1)}, f32[6,4,6]{2,1,0:T(4,128)S(1)}, f32[6,4,6,128]{3,2,1,0:T(8,128)S(1)}, f32[15,6,4,6]{3,2,1,0:T(4,128...) while((s32[]{:T(128)}, f32[6,4,6]{2,1,0:T(4,128)S(1)}, ...), condition=%wide.region_3.4_spmd, body=%wide.region_2.3_spmd.sunk | while | flops 56162 | bytes 374501 | solution.py:20
  60.4 0.9 constant_dynamic-slice_fusion.2
  61.3 0.1 fusion.70
  61.5 0.9 constant_dynamic-slice_fusion.2
  62.4 0.1 fusion.70
  62.6 0.9 constant_dynamic-slice_fusion.2
  63.5 0.1 fusion.70
  63.7 0.9 constant_dynamic-slice_fusion.2
  64.6 0.1 fusion.70
  64.8 0.9 constant_dynamic-slice_fusion.2
  65.7 0.1 fusion.70
  65.9 0.9 constant_dynamic-slice_fusion.2
  66.8 0.1 fusion.70
  67.0 0.9 constant_dynamic-slice_fusion.2
  67.9 0.1 fusion.70
  68.0 0.9 constant_dynamic-slice_fusion.2
  68.9 0.1 fusion.70
  69.1 0.9 constant_dynamic-slice_fusion.2
  70.0 0.1 fusion.70
  70.2 0.9 constant_dynamic-slice_fusion.2
  71.3 0.9 constant_dynamic-slice_fusion.2
  72.2 0.1 fusion.70
  72.4 0.9 constant_dynamic-slice_fusion.2
  73.3 0.1 fusion.70
  73.5 0.9 constant_dynamic-slice_fusion.2
  74.6 0.9 constant_dynamic-slice_fusion.2
  75.5 0.1 fusion.70
  75.7 0.9 constant_dynamic-slice_fusion.2
  76.6 0.1 fusion.70
  76.9 0.4 fusion.50
  77.3 8.1 %all-reduce = f32[6,384]{1,0:T(8,128)S(1)} all-reduce(f32[6,384]{1,0:T(8,128)S(1)} %fusion.50), channel_id=5, replica_groups=mesh['seq'=16,'exp'=2] {'exp'}, use_global_device_ids=true, to_apply=%region_4.5.clone | all-reduce | flops 2304 | bytes 18432
  85.6 1.1 collective-permute-done
  86.7 1.8 collective-permute-start.1
  88.5 1.8 collective-permute-done.1
  90.3 3.6 %collective-permute-done.2 = f32[3]{0:T(128)S(1)} collective-permute-done((f32[3]{0:T(128)S(1)}, f32[3]{0:T(128)S(1)}, u32[]{:S(2)}, u32[]{:S(2)}) %collective-permute-start.2) | collective-permute-done | bytes 44 | tf_op jit(solution)/shard_map/ppermute | solution.py:88
  93.9 4.5 %collective-permute-done.3 = f32[3]{0:T(128)S(1)} collective-permute-done((f32[3]{0:T(128)S(1)}, f32[3]{0:T(128)S(1)}, u32[]{:S(2)}, u32[]{:S(2)}) %collective-permute-start.3) | collective-permute-done | bytes 44 | tf_op jit(solution)/shard_map/ppermute | solution.py:88
  98.4 0.2 fusion.26
  98.6 0.3 select_reduce_fusion
  98.8 29.5 %psum.7 = f32[3,8]{1,0:T(4,128)S(1)} all-reduce(f32[3,8]{1,0:T(4,128)S(1)} %fusion.26), channel_id=1, replica_groups=mesh['seq'=16,'exp'=2] {'seq'}, use_global_device_ids=true, to_apply=%region_9.10 | all-reduce | flops 24 | bytes 192 | tf_op jit(solution)/shard_map/psum | solution.py:90
  128.3 0.2 fusion.30
  128.6 0.3 fusion.19
  128.9 0.2 convolution_convert_fusion
  129.1 6.3 %all_to_all.36 = bf16[8,3,384]{2,1,0:T(4,128)(2,1)S(1)} all-to-all(bf16[8,3,384]{2,1,0:T(4,128)(2,1)S(1)} %copy.33), channel_id=1, replica_groups=mesh['seq'=16,'exp'=2] {'exp'}, dimensions={0} | all-to-all | bytes 36864 | tf_op jit(solution)/shard_map/all_to_all | solution.py:113
  135.4 18.3 %all_gather.27 = bf16[4,6,6144]{2,1,0:T(8,128)(2,1)S(1)} all-gather(bf16[4,6,384]{2,1,0:T(8,128)(2,1)S(1)} %copy.35), channel_id=1, replica_groups=mesh['seq'=16,'exp'=2] {'seq'}, dimensions={2}, use_global_device_ids=true | all-gather | bytes 313344 | tf_op jit(solution)/shard_map/all_gather | solution.py:114
  153.7 9.9 %fusion.51 = f32[4,6,512]{2,1,0:T(8,128)S(1)} fusion(bf16[4,6,6144]{2,1,0:T(8,128)(2,1)S(1)} %all_gather.27, bf16[4,6144,512]{2,1,0:T(8,128)(2,1)} %param.25), kind=kOutput, calls=%fused_computation.70 | convolution fusion | flops 150994944 | bytes 25509888 | tf_op jit(solution)/shard_map/ern,enf->erf/dot_general | solution.py:115
  163.6 9.9 %fusion.16 = bf16[4,6,512]{2,1,0:T(8,128)(2,1)S(1)} fusion(bf16[4,6,6144]{2,1,0:T(8,128)(2,1)S(1)} %all_gather.27, bf16[4,6144,512]{2,1,0:T(8,128)(2,1)} %param.26, f32[4,6,512]{2,1,0:T(8,128)S(1)} %fusion.51), kind=kOutput, calls=%fused_computation.19 | convolution fusion | flops 151068672 | bytes 25534464 | tf_op jit(solution)/shard_map/ern,enf->erf/dot_general | solution.py:116
  173.5 10.9 %fusion.52 = f32[4,6,6144]{2,1,0:T(8,128)} fusion(bf16[4,6,512]{2,1,0:T(8,128)(2,1)S(1)} %fusion.16, bf16[4,512,6144]{2,1,0:T(8,128)(2,1)} %param.27), kind=kOutput, calls=%fused_computation.71 | convolution fusion | flops 150994944 | bytes 25780224 | tf_op jit(solution)/shard_map/erf,efd->erd/dot_general | solution.py:118
  184.5 54.9 %reduce-scatter.2.cloned.1.call-done = f32[4,6,384]{2,1,0:T(8,128)} async-done(((f32[4,6,6144]{2,1,0:T(8,128)}), f32[4,6,384]{2,1,0:T(8,128)}) %reduce-scatter.2.cloned.1.call-update) | async-done | bytes 36880 | tf_op jit(solution)/shard_map/reduce_scatter | solution.py:122
  239.3 1.4 copy.36
  240.8 3.3 %all-to-all-start.1 = ((f32[4,6,384]{2,0,1:T(4,128)}), f32[4,6,384]{2,0,1:T(4,128)S(1)}, u32[]{:S(2)}, u32[]{:S(2)}) async-start(f32[4,6,384]{2,0,1:T(4,128)} %copy.36), calls=%async_computation.2 | async-start | bytes 73728 | tf_op jit(solution)/shard_map/all_to_all | solution.py:123
  244.0 0.3 convolution_bitcast_fusion.1
  244.3 3.7 %all-to-all-done.1 = f32[4,6,384]{2,0,1:T(4,128)S(1)} async-done(((f32[4,6,384]{2,0,1:T(4,128)}), f32[4,6,384]{2,0,1:T(4,128)S(1)}, u32[]{:S(2)}, u32[]{:S(2)}) %all-to-all-start.1) | async-done | bytes 36896 | tf_op jit(solution)/shard_map/all_to_all | solution.py:123
  248.0 0.8 fusion.18
  (69 shorter events, 1.8 us)
Async XLA Ops:
  6.5 2.5 copy-start
  6.5 50.6 %all-gather.5.cloned.1.call-start = ((), (), s32[]{:S(2)}) async-start(), calls=%async_computation.4 | async-start | bytes 1253376 | tf_op jit(solution)/shard_map/all_gather | solution.py:17
  8.2 2.7 %copy-start.2 = (bf16[6,512,512]{2,1,0:T(8,128)(2,1)S(1)}, bf16[6,512,512]{2,1,0:T(8,128)(2,1)}, u32[]{:S(2)}) copy-start(bf16[6,512,512]{2,1,0:T(8,128)(2,1)} %param.18) | copy-start | bytes 9437188
  10.9 44.5 %copy-start.5 = (s32[3,2]{0,1:T(2,128)S(1)}, s32[3,2]{0,1:T(2,128)}, u32[]{:S(2)}) copy-start(s32[3,2]{0,1:T(2,128)} %param.23) | copy-start | bytes 76
  10.9 44.6 %copy-start.9 = (u32[32]{0:T(128)S(1)}, u32[32]{0:T(128)}, u32[]{:S(2)}) copy-start(u32[32]{0:T(128)} %constant.44) | copy-start | bytes 388
  13.0 226.3 %reduce-scatter.2.cloned.1.call-start = ((), (), s32[]{:S(2)}) async-start(), calls=%async_computation.3 | async-start | bytes 835584 | tf_op jit(solution)/shard_map/reduce_scatter | solution.py:122
  37.0 39.9 %copy-start.3 = (bf16[3072,384]{1,0:T(8,128)(2,1)S(1)}, bf16[3072,384]{1,0:T(8,128)(2,1)}, u32[]{:S(2)}) copy-start(bf16[3072,384]{1,0:T(8,128)(2,1)} %param.20) | copy-start | bytes 7077892
  60.4 25.0 %copy-start.4 = (bf16[3,384]{1,0:T(4,128)(2,1)S(1)}, bf16[3,384]{1,0:T(4,128)(2,1)}, u32[]{:S(2)}) copy-start(bf16[3,384]{1,0:T(4,128)(2,1)} %param.15) | copy-start | bytes 6916
  60.4 38.0 %copy-start.7 = (bf16[384,8]{0,1:T(8,128)(2,1)S(1)}, bf16[384,8]{0,1:T(8,128)(2,1)}, u32[]{:S(2)}) copy-start(bf16[384,8]{0,1:T(8,128)(2,1)} %param.22) | copy-start | bytes 18436
  60.4 38.0 %copy-start.8 = (f32[384]{0:T(512)S(1)}, f32[384]{0:T(512)}, u32[]{:S(2)}) copy-start(f32[384]{0:T(512)} %param.21) | copy-start | bytes 4612
  60.4 38.2 %copy-start.6 = (s32[8]{0:T(128)S(1)}, s32[8]{0:T(128)}, u32[]{:S(2)}) copy-start(s32[8]{0:T(128)} %param.24) | copy-start | bytes 100
  85.5 1.2 collective-permute-start
  86.7 3.6 %collective-permute-start.1 = (f32[3]{0:T(128)S(1)}, f32[3]{0:T(128)S(1)}, u32[]{:S(2)}, u32[]{:S(2)}) collective-permute-start(f32[3]{0:T(128)S(1)} %add.56), channel_id=1, source_target_pairs={{0,4},{2,6},{4,0},{6,2},{8,12},{10,14},{12,8},{14,10},{16,20},{18,... | collective-permute-start | bytes 44 | tf_op jit(solution)/shard_map/ppermute | solution.py:88
  90.3 3.6 %collective-permute-start.2 = (f32[3]{0:T(128)S(1)}, f32[3]{0:T(128)S(1)}, u32[]{:S(2)}, u32[]{:S(2)}) collective-permute-start(f32[3]{0:T(128)S(1)} %add.57), channel_id=1, source_target_pairs={{0,8},{2,10},{4,12},{6,14},{8,0},{10,2},{12,4},{14,6},{16,24},{18,... | collective-permute-start | bytes 44 | tf_op jit(solution)/shard_map/ppermute | solution.py:88
  93.9 4.5 %collective-permute-start.3 = (f32[3]{0:T(128)S(1)}, f32[3]{0:T(128)S(1)}, u32[]{:S(2)}, u32[]{:S(2)}) collective-permute-start(f32[3]{0:T(128)S(1)} %add.58), channel_id=1, source_target_pairs={{0,16},{2,18},{4,20},{6,22},{8,24},{10,26},{12,28},{14,30},{16,0},... | collective-permute-start | bytes 44 | tf_op jit(solution)/shard_map/ppermute | solution.py:88
  173.5 75.3 %copy-start.1 = (bf16[6,512,512]{2,1,0:T(8,128)(2,1)S(1)}, bf16[6,512,512]{2,1,0:T(8,128)(2,1)}, u32[]{:S(2)}) copy-start(bf16[6,512,512]{2,1,0:T(8,128)(2,1)} %param.17) | copy-start | bytes 9437188
  240.8 7.2 %all-to-all-start.1 = ((f32[4,6,384]{2,0,1:T(4,128)}), f32[4,6,384]{2,0,1:T(4,128)S(1)}, u32[]{:S(2)}, u32[]{:S(2)}) async-start(f32[4,6,384]{2,0,1:T(4,128)} %copy.36), calls=%async_computation.2 | async-start | bytes 73728 | tf_op jit(solution)/shard_map/all_to_all | solution.py:123
Sparse Core Ops, SparseCore 0:
  13.1 41.2 all-gather.4
  184.6 54.6 reduce-scatter.1
